TPU v7x, 16 devices: a whole 2x2x2 slice. The times are simulated.
16 devices in a mesh: rep: 1, dp: 16 (over x, y, z, core).
Axes of the slice: x: 2, y: 2, z: 2, core: 2. Of those that a mesh axis runs over, the one named last changes fastest.
Arguments:
- g_w_gate: bfloat16 [16, 2, 1024, 3328], P(('rep', 'dp'))
- g_w_up: bfloat16 [16, 2, 1024, 3328], P(('rep', 'dp'))
- g_w_down: bfloat16 [16, 2, 3328, 1024], P(('rep', 'dp'))
- w_gate: bfloat16 [2, 1024, 3328], replicated
- w_up: bfloat16 [2, 1024, 3328], replicated
- w_down: bfloat16 [2, 3328, 1024], replicated
- m_w_gate: float32 [2, 1024, 3328], P(None, 'dp')
- m_w_up: float32 [2, 1024, 3328], P(None, 'dp')
- m_w_down: float32 [2, 3328, 1024], P(None, 'dp')
- v_w_gate: float32 [2, 1024, 3328], P(None, 'dp')
- v_w_up: float32 [2, 1024, 3328], P(None, 'dp')
- v_w_down: float32 [2, 3328, 1024], P(None, 'dp')
Outputs:
- output 1: bfloat16 [2, 1024, 3328], P('rep')
- output 2: bfloat16 [2, 1024, 3328], P('rep')
- output 3: bfloat16 [2, 3328, 1024], P('rep')
- output 4: float32 [2, 1024, 3328], P('rep', 'dp')
- output 5: float32 [2, 1024, 3328], P('rep', 'dp')
- output 6: float32 [2, 3328, 1024], P('rep', 'dp')
- output 7: float32 [2, 1024, 3328], P('rep', 'dp')
- output 8: float32 [2, 1024, 3328], P('rep', 'dp')
- output 9: float32 [2, 3328, 1024], P('rep', 'dp')
All inputs are finite; a program needn't handle non-finite values.
Results may differ from a plain program's by a relative error of at most 0.022.
Values are sent between devices in bfloat16 or wider.
A program may use at most 2 GiB of HBM per device.

v0:
```python
import jax
import jax.numpy as jnp
from jax import lax
from jax.sharding import PartitionSpec as P


def adamw(w, m, v, g):
    m = 0.9 * m + 0.1 * g
    v = 0.95 * v + 0.05 * g * g
    step = m * lax.rsqrt(v + 1e-8) + 0.1 * w
    return (w - 0.02 * step).astype(jnp.bfloat16), m, v


def clipped(gradients, sum_of_squares, count):
    factor = jnp.minimum(1.0, 0.5 * lax.rsqrt(sum_of_squares / count + 1e-30))
    return [g * factor for g in gradients]


def solution(mesh):
    def step(*arrays):
        terms, weights, m, v = (arrays[i : i + 3] for i in (0, 3, 6, 9))
        gradients = [lax.psum_scatter(t[0], "dp", scatter_dimension=1, tiled=True).astype(jnp.float32) for t in terms]
        squares = lax.psum(sum(jnp.sum(g * g) for g in gradients), "dp")
        gradients = clipped(gradients, squares, lax.psum(1, "dp") * sum(g.size for g in gradients))
        me = lax.axis_index("dp")
        own = [lax.dynamic_slice_in_dim(w, me * one.shape[1], one.shape[1], 1).astype(jnp.float32) for w, one in zip(weights, m, strict=True)]
        new = [adamw(w, m, v, g) for w, m, v, g in zip(own, m, v, gradients, strict=True)]
        whole = [lax.all_gather(one[0], "dp", axis=1, tiled=True) for one in new]
        return (*whole, *(one[1] for one in new), *(one[2] for one in new))

    all_of, cut = P(None, None, None), P(None, "dp", None)
    return jax.shard_map(
        step,
        mesh=mesh,
        in_specs=(P(("rep", "dp"), None, None, None),) * 3 + (all_of,) * 3 + (cut,) * 6,
        out_specs=(P("rep", None, None),) * 3 + (P("rep", "dp", None),) * 6,
        check_vma=False,
    )
```

profile of v0, /device:TPU:0, one launch (start us, length us, event | category | flops | bytes accessed | tf_op | source)
XLA Modules:
  0.0 728.5 jit_solution(10926207655062337008)
XLA Ops:
  7.2 0.0 reduce-scatter.4.cloned.1.call-start
  7.2 0.7 reduce-scatter.4.cloned.1.call-update
  7.9 0.0 reduce-scatter.6.cloned.1.call-start
  8.0 0.7 reduce-scatter.6.cloned.1.call-update
  8.7 0.0 reduce-scatter.8.cloned.1.call-start
  8.7 0.7 reduce-scatter.8.cloned.1.call-update
  9.4 0.0 copy-start.3
  9.4 0.0 all-gather.8.cloned.1.call-start
  9.5 144.1 %reduce-scatter.4.cloned.1.call-done = bf16[2,64,3328]{2,1,0:T(8,128)(2,1)} async-done(((bf16[2,1024,3328]{2,1,0:T(8,128)(2,1)}), bf16[2,64,3328]{2,1,0:T(8,128)(2,1)}) %reduce-scatter.4.cloned.1.call-update) | async-done | bytes 851984 | tf_op jit(solution)/shard_map/reduce_scatter | solution.py:22
  153.6 2.2 fusion.9
  155.8 144.4 %reduce-scatter.6.cloned.1.call-done = bf16[2,64,3328]{2,1,0:T(8,128)(2,1)} async-done(((bf16[2,1024,3328]{2,1,0:T(8,128)(2,1)}), bf16[2,64,3328]{2,1,0:T(8,128)(2,1)}) %reduce-scatter.6.cloned.1.call-update) | async-done | bytes 851984 | tf_op jit(solution)/shard_map/reduce_scatter | solution.py:22
  300.2 2.2 fusion.10
  303.6 143.1 %reduce-scatter.8.cloned.1.call-done = bf16[2,208,1024]{2,1,0:T(8,128)(2,1)} async-done(((bf16[2,3328,1024]{2,1,0:T(8,128)(2,1)}), bf16[2,208,1024]{2,1,0:T(8,128)(2,1)}) %reduce-scatter.8.cloned.1.call-update) | async-done | bytes 851984 | tf_op jit(solution)/shard_map/reduce_scatter | solution.py:22
  446.7 2.2 fusion.11
  449.6 35.7 %psum.7 = f32[]{:T(128)} all-reduce(f32[]{:T(128)S(6)} %add.65), channel_id=1, replica_groups=mesh['rep'=1,'dp'=16] {'dp'}, use_global_device_ids=true, to_apply=%region_6.0 | all-reduce | flops 1 | bytes 8 | tf_op jit(solution)/shard_map/psum | solution.py:23
  486.0 0.0 copy-done.3
  486.0 0.0 copy-start.2
  486.0 4.6 fusion.17
  490.6 0.0 all-gather.8.cloned.1.call-update
  490.6 0.0 all-gather.4.cloned.1.call-start
  490.7 0.0 copy-done.2
  490.7 0.0 copy-start.1
  490.7 4.8 fusion.8
  495.5 0.0 all-gather.4.cloned.1.call-update
  495.5 0.0 all-gather.6.cloned.1.call-start
  495.6 0.0 copy-done.1
  495.6 4.7 fusion.14
  500.3 0.0 all-gather.6.cloned.1.call-update
  500.3 57.1 %all-gather.8.cloned.1.call-done = bf16[2,3328,1024]{2,1,0:T(8,128)(2,1)} async-done(((bf16[2,208,1024]{2,1,0:T(8,128)(2,1)}), bf16[2,3328,1024]{2,1,0:T(8,128)(2,1)}) %all-gather.8.cloned.1.call-update) | async-done | bytes 13631504 | tf_op jit(solution)/shard_map/all_gather | solution.py:28
  557.4 68.5 %all-gather.4.cloned.1.call-done = bf16[2,1024,3328]{2,1,0:T(8,128)(2,1)} async-done(((bf16[2,64,3328]{2,1,0:T(8,128)(2,1)}), bf16[2,1024,3328]{2,1,0:T(8,128)(2,1)}) %all-gather.4.cloned.1.call-update) | async-done | bytes 13631504 | tf_op jit(solution)/shard_map/all_gather | solution.py:28
  625.9 68.5 %all-gather.6.cloned.1.call-done = bf16[2,1024,3328]{2,1,0:T(8,128)(2,1)} async-done(((bf16[2,64,3328]{2,1,0:T(8,128)(2,1)}), bf16[2,1024,3328]{2,1,0:T(8,128)(2,1)}) %all-gather.6.cloned.1.call-update) | async-done | bytes 13631504 | tf_op jit(solution)/shard_map/all_gather | solution.py:28
  694.4 0.0 copy-start
  694.4 0.0 slice-start
  694.4 0.0 slice-start.1
  694.4 15.1 %copy.24 = bf16[2,1024,3328]{2,1,0:T(8,128)(2,1)} copy(bf16[2,1024,3328]{2,1,0:T(8,128)(2,1)} %all-gather.4.cloned.1.call-done) | data formatting | bytes 27262976
  709.4 0.0 copy-done
  709.4 0.0 slice-start.2
  709.4 0.0 slice-start.3
  709.4 6.6 copy.25
  716.0 0.0 slice-done
  716.0 0.0 slice-done.1
  716.0 0.0 slice-done.2
  716.0 0.5 slice-done.3
  716.5 5.1 copy.26
  (1 shorter events, 0.0 us)
Async XLA Ops:
  7.2 146.4 %reduce-scatter.4.cloned.1.call-start = ((), (), s32[]{:S(2)}) async-start(), calls=%async_computation.3 | async-start | bytes 14483456 | tf_op jit(solution)/shard_map/reduce_scatter | solution.py:22
  7.9 292.2 %reduce-scatter.6.cloned.1.call-start = ((), (), s32[]{:S(2)}) async-start(), calls=%async_computation.4 | async-start | bytes 14483456 | tf_op jit(solution)/shard_map/reduce_scatter | solution.py:22
  8.7 438.1 %reduce-scatter.8.cloned.1.call-start = ((), (), s32[]{:S(2)}) async-start(), calls=%async_computation.5 | async-start | bytes 14483456 | tf_op jit(solution)/shard_map/reduce_scatter | solution.py:22
  9.4 476.6 %copy-start.3 = (f32[2,208,1024]{2,1,0:T(8,128)S(1)}, f32[2,208,1024]{2,1,0:T(8,128)}, u32[]{:S(2)}) copy-start(f32[2,208,1024]{2,1,0:T(8,128)} %param.23) | copy-start | bytes 5111812
  9.4 548.0 %all-gather.8.cloned.1.call-start = ((), (), s32[]{:S(2)}) async-start(), calls=%async_computation.8 | async-start | bytes 14483456 | tf_op jit(solution)/shard_map/all_gather | solution.py:28
  486.0 4.7 copy-start.2
  490.6 135.2 %all-gather.4.cloned.1.call-start = ((), (), s32[]{:S(2)}) async-start(), calls=%async_computation.6 | async-start | bytes 14483456 | tf_op jit(solution)/shard_map/all_gather | solution.py:28
  490.7 4.9 copy-start.1
  495.5 198.9 %all-gather.6.cloned.1.call-start = ((), (), s32[]{:S(2)}) async-start(), calls=%async_computation.7 | async-start | bytes 14483456 | tf_op jit(solution)/shard_map/all_gather | solution.py:28
  694.4 15.1 %copy-start = (bf16[2,1024,3328]{2,1,0:T(8,128)(2,1)S(1)}, bf16[2,1024,3328]{2,1,0:T(8,128)(2,1)}, u32[]{:S(2)}) copy-start(bf16[2,1024,3328]{2,1,0:T(8,128)(2,1)} %all-gather.6.cloned.1.call-done) | copy-start | bytes 40894468
  694.4 21.6 %slice-start = ((s8[13631488]{0:T(1024)(128)(4,1)}), s8[4194304]{0:T(1024)(128)(4,1)S(1)}, s32[]{:S(2)}) async-start(s8[13631488]{0:T(1024)(128)(4,1)} %bitcast.6), calls=%async_computation.9 | async-start | bytes 8388608
  694.4 21.6 %slice-start.1 = ((s8[13631488]{0:T(1024)(128)(4,1)}), s8[4194304]{0:T(1024)(128)(4,1)S(1)}, s32[]{:S(2)}) async-start(s8[13631488]{0:T(1024)(128)(4,1)} %bitcast.6), calls=%async_computation.10 | async-start | bytes 8388608
  709.4 6.6 slice-start.2
  709.4 7.1 slice-start.3
Sparse Core Ops, SparseCore 0:
  10.3 143.2 reduce-scatter.3
  155.8 144.2 reduce-scatter.5
  302.4 144.2 reduce-scatter.7
  490.8 66.5 all-gather.7
  560.1 65.7 all-gather.3
  628.6 65.7 all-gather.5
where the time goes:
time: 729 us; the launch traced here: 728 us
  waiting for transfers between devices  628 us (86%)
  blocking collectives  35.7 us (5%)
  local copies, waits for them, and re-layouts  27.3 us (4%)
  other arithmetic  20.7 us (3%)
  between operations  16.8 us (2%)
    reduce_scatter x3, waiting for transfers between devices, step(): lax.psum_scatter(t[0], 'dp', scatter_dimension=1, tiled=True)  432 us
    all_gather x3, waiting for transfers between devices, step(): whole = [lax.all_gather(one[0], 'dp', axis=1, tiled=True) for one in new]  194 us
    psum x1, blocking collectives, step(): squares = lax.psum(sum((jnp.sum(g * g) for g in gradients)), 'dp')  35.7 us
    unnamed x19, local copies, waits for them, and re-layouts  27.3 us
  transfers between devices with their start and end apart: 6, of which 6 were waited for; matrix products, arithmetic and copies ran while one was open for 2% of the time, Pallas kernels for 0%

commit v1 on v0

v1 whole, which is shorter than its diff:
```python
import functools

import jax
import jax.numpy as jnp
from jax import lax
from jax.experimental import pallas as pl
from jax.experimental.pallas import tpu as pltpu
from jax.sharding import PartitionSpec as P

DEVICES = 16
LAYERS = 2
WINDOW = 12
BF16, F32 = jnp.bfloat16, jnp.float32
AXES = ((0, 1, 2), (1, 2, 0), (2, 0, 1))
UNITS = [(layer, w) for layer in range(LAYERS) for w in range(3)]


def gather_order():
    free, events, order = [0.0, 0.0, 0.0], [], []

    def send(now, layer, w, block):
        for bit in (0, 1, 2):
            if block >> bit:
                continue
            axis = AXES[w][2 - bit]
            free[axis] = max(free[axis], now) + 1.0
            events.append((free[axis], layer, w, block | 1 << bit))

    for i, (layer, w) in enumerate(UNITS):
        send(0.01 * i, layer, w, 0)
    while events:
        events.sort()
        now, layer, w, block = events.pop(0)
        order.append((layer, w, block))
        send(now + 0.1, layer, w, block)
    return order


def adamw(w, m, v, g):
    m = 0.9 * m + 0.1 * g
    v = 0.95 * v + 0.05 * g * g
    step = m * lax.rsqrt(v + 1e-8) + 0.1 * w
    return (w - 0.02 * step).astype(BF16), m, v


def tiles(rows, columns, body, init=None):
    def step(i, carry):
        for c in range(0, columns, 256):
            carry = body(pl.ds(pl.multiple_of(i * 16, 16), 16), pl.ds(c, 256), carry)
        return carry

    return lax.fori_loop(0, rows // 16, step, init)


def step_kernel(count, *refs):
    g, wt, m_in, v_in = (refs[i : i + 3] for i in (0, 3, 6, 9))
    out, m, v = (refs[i : i + 3] for i in (12, 15, 18))
    got2, got3, own_w = (refs[i : i + 3] for i in (21, 24, 27))
    squares, all_squares, send_sem, recv_sem, load_sem, in_sem, sum_send, sum_recv = refs[30:]
    rows = [ref.shape[2] // DEVICES for ref in g]
    columns = [ref.shape[3] for ref in g]

    me = lax.axis_index("dp")
    core = lax.rem(me, 2)
    bits = (me // 8, lax.rem(me // 4, 2), lax.rem(me // 2, 2))
    hop = [(1 - 2 * b) * s for b, s in zip(bits, (8, 4, 2), strict=True)]
    other = 1 - 2 * core

    def away(w, slot):
        return sum(hop[AXES[w][2 - bit]] for bit in range(3) if slot >> bit & 1)

    def block(w, index):
        return pl.ds(pl.multiple_of(index * rows[w], rows[w]), rows[w])

    def part(w, layer, unit):
        return out[w].at[layer, unit * rows[w] : (unit + 1) * rows[w]]

    def copy(w, layer, n, source, target, to):
        return pltpu.make_async_remote_copy(
            src_ref=source,
            dst_ref=target,
            send_sem=send_sem.at[layer * 3 + w, n],
            recv_sem=recv_sem.at[layer * 3 + w, n],
            device_id={"dp": me + to},
            device_id_type=pl.DeviceIdType.MESH,
        )

    def load(w, layer, slot):
        source = g[w].at[0, layer, block(w, me + away(w, slot))]
        return pltpu.make_async_copy(source, part(w, layer, slot + 4), load_sem.at[layer * 3 + w, slot])

    def swap(w, layer, slot):
        source = g[w].at[0, layer, block(w, me + other + away(w, slot))]
        return copy(w, layer, slot, source, part(w, layer, slot), other)

    def first(w, layer, slot):
        return copy(w, layer, 8 + slot - 4, part(w, layer, 4 + slot), part(w, layer, 8 + slot), hop[AXES[w][0]])

    def second(w, layer, slot):
        return copy(w, layer, 12 + slot - 2, part(w, layer, slot), got2[w].at[layer, slot - 2], hop[AXES[w][1]])

    def third(w, layer):
        return copy(w, layer, 14, part(w, layer, 1), got3[w].at[layer], hop[AXES[w][2]])

    early = [(w, layer, slot) for layer in range(LAYERS) for slot in (7, 6, 5, 4) for w in range(3)]
    late = [(w, layer, slot) for pair in ((3, 2), (1,), (0,)) for layer in range(LAYERS) for slot in pair for w in range(3)]
    for unit in early:
        load(*unit).start()

    barrier = pltpu.get_barrier_semaphore()
    for to in (other, *hop):
        pl.semaphore_signal(barrier, inc=1, device_id={"dp": me + to}, device_id_type=pl.DeviceIdType.MESH)
    pl.semaphore_wait(barrier, 4)

    swaps = [swap(*unit) for unit in early + late]
    for c in swaps[:WINDOW]:
        c.start()

    def total(w, sources, target):
        def tile(r, c, carry):
            acc = sources[0][r, c].astype(F32)
            for s in sources[1:]:
                acc += s[r, c].astype(F32)
            target[r, c] = acc.astype(BF16)
            return carry

        tiles(rows[w], columns[w], tile)

    for i, (w, layer, slot) in enumerate(early):
        load(w, layer, slot).wait()
        swaps[i].wait_recv()
        total(w, [part(w, layer, 4 + slot), part(w, layer, slot)], part(w, layer, 4 + slot))
        first(w, layer, slot).start()
        load(w, layer, slot - 4).start()
        if i + WINDOW < len(swaps):
            swaps[i + WINDOW].start()

    moments = [
        pltpu.make_async_copy(source[w].at[:, block(w, me)] if source is wt else source[w], target[w], in_sem.at[w, k])
        for w in range(3)
        for k, (source, target) in enumerate(((m_in, m), (v_in, v), (wt, own_w)))
    ]
    for c in moments:
        c.start()

    squares[...] = jnp.zeros_like(squares)
    for i, (w, layer, slot) in enumerate(late, len(early)):
        load(w, layer, slot).wait()
        swaps[i].wait_recv()
        first(w, layer, slot + 4).wait_recv()
        sources = [part(w, layer, slot + 4), part(w, layer, slot), part(w, layer, 12 + slot)]
        if slot < 2:
            second(w, layer, slot + 2).wait_recv()
            sources.append(got2[w].at[layer, slot])
        if slot == 0:
            third(w, layer).wait_recv()
            last = got3[w].at[layer]
            sources.append(last)

            def tile(r, c, carry, sources=sources, last=last):
                acc = sources[0][r, c].astype(F32)
                for s in sources[1:]:
                    acc += s[r, c].astype(F32)
                rounded = acc.astype(BF16)
                last[r, c] = rounded
                rounded = rounded.astype(F32)
                return carry + rounded * rounded

            squares[...] += tiles(rows[w], columns[w], tile, jnp.zeros((16, 256), F32))
        else:
            total(w, sources, part(w, layer, slot))
            (third(w, layer) if slot == 1 else second(w, layer, slot)).start()
        if i + WINDOW < len(swaps):
            swaps[i + WINDOW].start()

    for c in swaps:
        c.wait_send()
    for w, layer, slot in early:
        first(w, layer, slot).wait_send()
    for w, layer, slot in late:
        if slot:
            (third(w, layer) if slot == 1 else second(w, layer, slot)).wait_send()

    everyone = [
        pltpu.make_async_remote_copy(
            src_ref=all_squares.at[0],
            dst_ref=all_squares.at[k],
            send_sem=sum_send.at[k],
            recv_sem=sum_recv.at[k],
            device_id={"dp": lax.rem(me + k, DEVICES)},
            device_id_type=pl.DeviceIdType.MESH,
        )
        for k in range(1, DEVICES)
    ]
    s = squares[...]
    s = s[:8] + s[8:]
    all_squares[0] = s[:, :128] + s[:, 128:]
    for c in everyone:
        c.start()
    for c in moments:
        c.wait()
    for c in everyone:
        c.wait_recv()
    s = jnp.sum(jnp.sum(jnp.sum(all_squares[...], axis=0), axis=0, keepdims=True), axis=1, keepdims=True)
    factor = jnp.minimum(1.0, 0.5 * lax.rsqrt(s / count + 1e-30))

    def forward(w, layer, k, bit):
        where = out[w].at[layer, block(w, me + away(w, k))]
        return copy(w, layer, 7 + k if bit == 3 else (k | 1 << bit) - 1, where, where, other if bit == 3 else hop[AXES[w][2 - bit]])

    def arrived(w, layer, k):
        bit = k.bit_length() - 1
        return copy(w, layer, k - 1, out[w].at[layer, block(w, me)], out[w].at[layer, block(w, me + away(w, k))], hop[AXES[w][2 - bit]])

    sent = []

    def pass_on(w, layer, k):
        for bit in range(4):
            if not k >> bit or bit == 3:
                sent.append(forward(w, layer, k, bit))
                sent[-1].start()

    for layer, w in UNITS:

        def tile(r, c, carry, layer=layer, w=w):
            grad = got3[w][layer, r, c].astype(F32) * factor
            new, m[w][layer, r, c], v[w][layer, r, c] = adamw(own_w[w][layer, r, c].astype(F32), m[w][layer, r, c], v[w][layer, r, c], grad)
            own_w[w][layer, r, c] = new
            at = pl.ds(pl.multiple_of(me * rows[w] + r.start, 16), 16)
            out[w][layer, at, c] = new
            return carry

        tiles(rows[w], columns[w], tile)
        pass_on(w, layer, 0)
    for layer, w, k in gather_order():
        arrived(w, layer, k).wait_recv()
        pass_on(w, layer, k)
    for layer, w in UNITS:
        for k in range(8):
            where = out[w].at[layer, block(w, me + other + away(w, k))]
            copy(w, layer, 7 + k, where, where, other).wait_recv()
    for c in sent:
        c.wait_send()
    for c in everyone:
        c.wait_send()


def write_kernel(*refs):
    sem = refs[18]
    copies = [pltpu.make_async_copy(refs[i].at[layer], refs[9 + i].at[layer], sem.at[i, layer]) for i in range(9) for layer in range(LAYERS)]
    for c in copies:
        c.start()
    for c in copies:
        c.wait()


def solution(mesh):
    def step(*arrays):
        weights, moments = arrays[3:6], arrays[6:12]
        blocks = [one.shape for one in moments[:3]]
        new = [pltpu.VMEM(w.shape, BF16) for w in weights] + [pltpu.VMEM(one.shape, F32) for one in moments]
        hbm, vmem = pl.BlockSpec(memory_space=pl.ANY), pl.BlockSpec(memory_space=pltpu.VMEM)
        dma = pltpu.SemaphoreType.DMA
        count = float(sum(w.size for w in weights))
        new = pl.pallas_call(
            functools.partial(step_kernel, count),
            out_shape=new,
            in_specs=[hbm] * 12,
            out_specs=[vmem] * 9,
            scratch_shapes=[
                *(pltpu.VMEM((LAYERS, 2, *b[1:]), BF16) for b in blocks),
                *(pltpu.VMEM(b, BF16) for b in blocks),
                *(pltpu.VMEM(b, BF16) for b in blocks),
                pltpu.VMEM((16, 256), F32),
                pltpu.VMEM((DEVICES, 8, 128), F32),
                dma((6, 15)),
                dma((6, 15)),
                dma((6, 8)),
                dma((3, 3)),
                dma((DEVICES,)),
                dma((DEVICES,)),
            ],
            compiler_params=pltpu.CompilerParams(collective_id=0, has_side_effects=True, vmem_limit_bytes=12 * 2**20),
            name="step",
        )(*arrays)
        return tuple(
            pl.pallas_call(
                write_kernel,
                out_shape=[jax.ShapeDtypeStruct(one.shape, one.dtype) for one in new],
                in_specs=[hbm] * 9,
                out_specs=[hbm] * 9,
                scratch_shapes=[dma((9, LAYERS))],
                compiler_params=pltpu.CompilerParams(vmem_limit_bytes=2**20),
                name="write",
            )(*new)
        )

    all_of, cut = P(None, None, None), P(None, "dp", None)
    return jax.shard_map(
        step,
        mesh=mesh,
        in_specs=(P(("rep", "dp"), None, None, None),) * 3 + (all_of,) * 3 + (cut,) * 6,
        out_specs=(P("rep", None, None),) * 3 + (P("rep", "dp", None),) * 6,
        check_vma=False,
    )
```

time: 729 us -> 324 us (0.44)
  waiting for transfers between devices: 628 us -> 0 us
  Pallas kernels: 0 us -> 293 us
  blocking collectives: 35.7 us -> 0 us
  other arithmetic: 20.7 us -> 0 us
  between operations: 16.8 us -> 0.67 us
    reduce_scatter x3 -> x0, waiting for transfers between devices: 432 us -> none  [step(): lax.psum_scatter(t[0], 'dp', scatter_dimension=1, tiled=True)]
    pallas_call x0 -> x2, Pallas kernels: none -> 293 us  [the longest x1 277 us: step(): pl.pallas_call(functools.partial(step_kernel, count), out_shape=new, in_s...]
    all_gather x3 -> x0, waiting for transfers between devices: 194 us -> none  [step(): whole = [lax.all_gather(one[0], 'dp', axis=1, tiled=True) for one in new]]
    psum x1 -> x0, blocking collectives: 35.7 us -> none  [step(): squares = lax.psum(sum((jnp.sum(g * g) for g in gradients)), 'dp')]
    convert_element_type x3 -> x0, other arithmetic: 14.1 us -> none  [adamw(): return ((w - 0.02 * step).astype(jnp.bfloat16), m, v)]
    unnamed x19 -> x12, local copies, waits for them, and re-layouts: 27.3 us -> 30 us
  transfers between devices with their start and end apart: 6 -> 0, of which waited for: 6 -> 0; matrix products, arithmetic and copies ran while one was open for 2% -> 0% of each run, Pallas kernels for 0% -> 0%
where the time goes in v1:
time: 324 us
  Pallas kernels  293 us (90%)
  local copies, waits for them, and re-layouts  30 us (9%)
    pallas_call x1, Pallas kernels, step(): pl.pallas_call(functools.partial(step_kernel, count), out_shape=new, in_s...  277 us
    unnamed x12, local copies, waits for them, and re-layouts  30 us
    pallas_call x1, Pallas kernels, step(): pl.pallas_call(write_kernel, out_shape=[jax.ShapeDtypeStruct(one.shape, o...  16.4 us

profile of v1, /device:TPU:0, one launch (start us, length us, event | category | flops | bytes accessed | tf_op | source)
XLA Modules:
  0.0 323.8 jit_solution(1686900271121281257)
XLA Ops:
  0.6 276.7 %step.1 = (bf16[2,1024,3328]{2,1,0:T(8,128)(2,1)S(1)}, bf16[2,1024,3328]{2,1,0:T(8,128)(2,1)S(1)}, bf16[2,3328,1024]{2,1,0:T(8,128)(2,1)S(1)}, f32[2,64,3328]{2,...) custom-call(bf16[1,2,1024,3328]{3,2,1,0:T(8,128)(2,1)} %refs_0_.1, ...), custom_call_target="tpu_custom_call" | custom-call | tf_op jit(solution)/shard_map/step/pallas_call | solution.py:265
  277.4 0.0 copy-start
  277.4 5.1 %copy-done = bf16[2,1024,3328]{2,1,0:T(8,128)(2,1)} copy-done((bf16[2,1024,3328]{2,1,0:T(8,128)(2,1)}, bf16[2,1024,3328]{2,1,0:T(8,128)(2,1)S(1)}, u32[]{:S(2)}) %copy-start) | copy-done | bytes 13631512
  282.5 0.0 copy-start.2
  282.5 5.1 %copy-done.2 = bf16[2,1024,3328]{2,1,0:T(8,128)(2,1)} copy-done((bf16[2,1024,3328]{2,1,0:T(8,128)(2,1)}, bf16[2,1024,3328]{2,1,0:T(8,128)(2,1)S(1)}, u32[]{:S(2)}) %copy-start.2) | copy-done | bytes 13631512
  287.6 0.0 copy-start.4
  287.6 5.1 %copy-done.4 = bf16[2,3328,1024]{2,1,0:T(8,128)(2,1)} copy-done((bf16[2,3328,1024]{2,1,0:T(8,128)(2,1)}, bf16[2,3328,1024]{2,1,0:T(8,128)(2,1)S(1)}, u32[]{:S(2)}) %copy-start.4) | copy-done | bytes 13631512
  292.8 0.0 copy-start.1
  292.8 4.9 %copy-done.1 = bf16[2,1024,3328]{2,1,0:T(8,128)(2,1)S(1)} copy-done((bf16[2,1024,3328]{2,1,0:T(8,128)(2,1)S(1)}, bf16[2,1024,3328]{2,1,0:T(8,128)(2,1)}, u32[]{:S(2)}) %copy-start.1) | copy-done | bytes 13631512
  297.6 0.0 copy-start.3
  297.6 4.9 %copy-done.3 = bf16[2,1024,3328]{2,1,0:T(8,128)(2,1)S(1)} copy-done((bf16[2,1024,3328]{2,1,0:T(8,128)(2,1)S(1)}, bf16[2,1024,3328]{2,1,0:T(8,128)(2,1)}, u32[]{:S(2)}) %copy-start.3) | copy-done | bytes 13631512
  302.5 0.0 copy-start.5
  302.5 4.9 %copy-done.5 = bf16[2,3328,1024]{2,1,0:T(8,128)(2,1)S(1)} copy-done((bf16[2,3328,1024]{2,1,0:T(8,128)(2,1)S(1)}, bf16[2,3328,1024]{2,1,0:T(8,128)(2,1)}, u32[]{:S(2)}) %copy-start.5) | copy-done | bytes 13631512
  307.4 16.4 %write.1 = (bf16[2,1024,3328]{2,1,0:T(8,128)(2,1)}, bf16[2,1024,3328]{2,1,0:T(8,128)(2,1)}, bf16[2,3328,1024]{2,1,0:T(8,128)(2,1)}, f32[2,64,3328]{2,1,0:T(8,128...) custom-call(bf16[2,1024,3328]{2,1,0:T(8,128)(2,1)S(1)} %copy-done.1,, ...), custom_call_target="tpu_custom_call" | custom-call | tf_op jit(solution)/shard_map/write/pallas_call | solution.py:287
Async XLA Ops:
  277.4 5.1 %copy-start = (bf16[2,1024,3328]{2,1,0:T(8,128)(2,1)}, bf16[2,1024,3328]{2,1,0:T(8,128)(2,1)S(1)}, u32[]{:S(2)}) copy-start(bf16[2,1024,3328]{2,1,0:T(8,128)(2,1)S(1)} %get-tuple-element.18.refs_0_) | copy-start | bytes 40894468
  282.5 5.1 %copy-start.2 = (bf16[2,1024,3328]{2,1,0:T(8,128)(2,1)}, bf16[2,1024,3328]{2,1,0:T(8,128)(2,1)S(1)}, u32[]{:S(2)}) copy-start(bf16[2,1024,3328]{2,1,0:T(8,128)(2,1)S(1)} %get-tuple-element.19.refs_1_) | copy-start | bytes 40894468
  287.6 5.1 %copy-start.4 = (bf16[2,3328,1024]{2,1,0:T(8,128)(2,1)}, bf16[2,3328,1024]{2,1,0:T(8,128)(2,1)S(1)}, u32[]{:S(2)}) copy-start(bf16[2,3328,1024]{2,1,0:T(8,128)(2,1)S(1)} %get-tuple-element.20.refs_2_) | copy-start | bytes 40894468
  292.8 4.9 %copy-start.1 = (bf16[2,1024,3328]{2,1,0:T(8,128)(2,1)S(1)}, bf16[2,1024,3328]{2,1,0:T(8,128)(2,1)}, u32[]{:S(2)}) copy-start(bf16[2,1024,3328]{2,1,0:T(8,128)(2,1)} %copy-done) | copy-start | bytes 40894468
  297.6 4.9 %copy-start.3 = (bf16[2,1024,3328]{2,1,0:T(8,128)(2,1)S(1)}, bf16[2,1024,3328]{2,1,0:T(8,128)(2,1)}, u32[]{:S(2)}) copy-start(bf16[2,1024,3328]{2,1,0:T(8,128)(2,1)} %copy-done.2) | copy-start | bytes 40894468
  302.5 4.9 %copy-start.5 = (bf16[2,3328,1024]{2,1,0:T(8,128)(2,1)S(1)}, bf16[2,3328,1024]{2,1,0:T(8,128)(2,1)}, u32[]{:S(2)}) copy-start(bf16[2,3328,1024]{2,1,0:T(8,128)(2,1)} %copy-done.4) | copy-start | bytes 40894468

commit v2 on v1

--- a/solution.py
+++ b/solution.py
@@ -55,8 +55,7 @@
 def step_kernel(count, *refs):
     g, wt, m_in, v_in = (refs[i : i + 3] for i in (0, 3, 6, 9))
     out, m, v = (refs[i : i + 3] for i in (12, 15, 18))
-    got2, got3, own_w = (refs[i : i + 3] for i in (21, 24, 27))
-    squares, all_squares, send_sem, recv_sem, load_sem, in_sem, sum_send, sum_recv = refs[30:]
+    wide, tall, squares, all_squares, send_sem, recv_sem, load_sem, in_sem, tile_sem, sum_send, sum_recv, free_sem = refs[21:]
     rows = [ref.shape[2] // DEVICES for ref in g]
     columns = [ref.shape[3] for ref in g]
 
@@ -97,10 +96,10 @@
         return copy(w, layer, 8 + slot - 4, part(w, layer, 4 + slot), part(w, layer, 8 + slot), hop[AXES[w][0]])
 
     def second(w, layer, slot):
-        return copy(w, layer, 12 + slot - 2, part(w, layer, slot), got2[w].at[layer, slot - 2], hop[AXES[w][1]])
+        return copy(w, layer, 12 + slot - 2, part(w, layer, slot), part(w, layer, 8 + slot), hop[AXES[w][1]])
 
     def third(w, layer):
-        return copy(w, layer, 14, part(w, layer, 1), got3[w].at[layer], hop[AXES[w][2]])
+        return copy(w, layer, 14, part(w, layer, 1), part(w, layer, 9), hop[AXES[w][2]])
 
     early = [(w, layer, slot) for layer in range(LAYERS) for slot in (7, 6, 5, 4) for w in range(3)]
     late = [(w, layer, slot) for pair in ((3, 2), (1,), (0,)) for layer in range(LAYERS) for slot in pair for w in range(3)]
@@ -135,48 +134,61 @@
         if i + WINDOW < len(swaps):
             swaps[i + WINDOW].start()
 
-    moments = [
-        pltpu.make_async_copy(source[w].at[:, block(w, me)] if source is wt else source[w], target[w], in_sem.at[w, k])
-        for w in range(3)
-        for k, (source, target) in enumerate(((m_in, m), (v_in, v), (wt, own_w)))
-    ]
-    for c in moments:
-        c.start()
+    loads = [pltpu.make_async_copy(m_in[w], m[w], in_sem.at[w, 0]) for w in range(3)]
+    for c in loads:
+        c.start()
+
+    def tile_load(w, layer, i, slot):
+        source = v_in[w].at[layer, pl.ds(pl.multiple_of(i * 16, 16), 16)]
+        return pltpu.make_async_copy(source, (tall if w == 2 else wide).at[slot], tile_sem.at[int(w == 2), slot])
+
+    for i in range(4):
+        tile_load(0, 0, i, i).start()
+        tile_load(2, 0, i, i).start()
 
     squares[...] = jnp.zeros_like(squares)
+    freed = set()
     for i, (w, layer, slot) in enumerate(late, len(early)):
+        if layer not in freed:
+            freed.add(layer)
+            for x in range(3):
+                for sent_slot in (7, 6, 5):
+                    first(x, layer, sent_slot).wait_send()
+                for axis in (1, 2):
+                    to = {"dp": me + hop[AXES[x][axis]]}
+                    pl.semaphore_signal(free_sem.at[layer * 3 + x, axis - 1], inc=1, device_id=to, device_id_type=pl.DeviceIdType.MESH)
         load(w, layer, slot).wait()
         swaps[i].wait_recv()
         first(w, layer, slot + 4).wait_recv()
         sources = [part(w, layer, slot + 4), part(w, layer, slot), part(w, layer, 12 + slot)]
         if slot < 2:
             second(w, layer, slot + 2).wait_recv()
-            sources.append(got2[w].at[layer, slot])
+            sources.append(part(w, layer, 10 + slot))
         if slot == 0:
             third(w, layer).wait_recv()
-            last = got3[w].at[layer]
-            sources.append(last)
-
-            def tile(r, c, carry, sources=sources, last=last):
+            sources.append(part(w, layer, 9))
+
+            def tile(r, c, carry, sources=sources, w=w, layer=layer):
                 acc = sources[0][r, c].astype(F32)
                 for s in sources[1:]:
                     acc += s[r, c].astype(F32)
-                rounded = acc.astype(BF16)
-                last[r, c] = rounded
-                rounded = rounded.astype(F32)
+                rounded = acc.astype(BF16).astype(F32)
+                v[w][layer, r, c] = rounded
                 return carry + rounded * rounded
 
             squares[...] += tiles(rows[w], columns[w], tile, jnp.zeros((16, 256), F32))
         else:
             total(w, sources, part(w, layer, slot))
+            if slot in (3, 1):
+                pl.semaphore_wait(free_sem.at[layer * 3 + w, int(slot == 1)], 1)
             (third(w, layer) if slot == 1 else second(w, layer, slot)).start()
         if i + WINDOW < len(swaps):
             swaps[i + WINDOW].start()
 
     for c in swaps:
         c.wait_send()
-    for w, layer, slot in early:
-        first(w, layer, slot).wait_send()
+    for layer, w in UNITS:
+        first(w, layer, 4).wait_send()
     for w, layer, slot in late:
         if slot:
             (third(w, layer) if slot == 1 else second(w, layer, slot)).wait_send()
@@ -197,7 +209,10 @@
     all_squares[0] = s[:, :128] + s[:, 128:]
     for c in everyone:
         c.start()
-    for c in moments:
+    loads += [pltpu.make_async_copy(wt[w].at[:, block(w, me)], out[w].at[:, block(w, me)], in_sem.at[w, 1]) for w in range(3)]
+    for c in loads[3:]:
+        c.start()
+    for c in loads:
         c.wait()
     for c in everyone:
         c.wait_recv()
@@ -220,17 +235,37 @@
                 sent.append(forward(w, layer, k, bit))
                 sent[-1].start()
 
+    def advance(w, layer, i):
+        slot = i if w < 2 else lax.rem(layer * (rows[w] // 16) + i, 4)
+        tile_load(w, layer, i, slot).wait()
+        r = pl.ds(pl.multiple_of(i * 16, 16), 16)
+        at = pl.ds(pl.multiple_of(me * rows[w] + i * 16, 16), 16)
+        for column in range(0, columns[w], 256):
+            c = pl.ds(column, 256)
+            old = (tall if w == 2 else wide)[slot, :, c]
+            new, m[w][layer, r, c], v[w][layer, r, c] = adamw(
+                out[w][layer, at, c].astype(F32), m[w][layer, r, c], old, v[w][layer, r, c] * factor
+            )
+            out[w][layer, at, c] = new
+        if w == 0:
+            tile_load(1, layer, i, slot).start()
+        elif w == 1 and layer + 1 < LAYERS:
+            tile_load(0, layer + 1, i, slot).start()
+        elif w == 2:
+            ahead = i + 4
+
+            @pl.when(ahead < rows[w] // 16)
+            def _():
+                tile_load(w, layer, ahead, slot).start()
+
+            if layer + 1 < LAYERS:
+
+                @pl.when(ahead >= rows[w] // 16)
+                def _():
+                    tile_load(w, layer + 1, ahead - rows[w] // 16, slot).start()
+
     for layer, w in UNITS:
-
-        def tile(r, c, carry, layer=layer, w=w):
-            grad = got3[w][layer, r, c].astype(F32) * factor
-            new, m[w][layer, r, c], v[w][layer, r, c] = adamw(own_w[w][layer, r, c].astype(F32), m[w][layer, r, c], v[w][layer, r, c], grad)
-            own_w[w][layer, r, c] = new
-            at = pl.ds(pl.multiple_of(me * rows[w] + r.start, 16), 16)
-            out[w][layer, at, c] = new
-            return carry
-
-        tiles(rows[w], columns[w], tile)
+        lax.fori_loop(0, rows[w] // 16, lambda i, _, w=w, layer=layer: advance(w, layer, i), None)
         pass_on(w, layer, 0)
     for layer, w, k in gather_order():
         arrived(w, layer, k).wait_recv()
@@ -259,7 +294,7 @@
         weights, moments = arrays[3:6], arrays[6:12]
         blocks = [one.shape for one in moments[:3]]
         new = [pltpu.VMEM(w.shape, BF16) for w in weights] + [pltpu.VMEM(one.shape, F32) for one in moments]
-        hbm, vmem = pl.BlockSpec(memory_space=pl.ANY), pl.BlockSpec(memory_space=pltpu.VMEM)
+        hbm, vmem = pl.BlockSpec(memory_space=pltpu.HBM), pl.BlockSpec(memory_space=pltpu.VMEM)
         dma = pltpu.SemaphoreType.DMA
         count = float(sum(w.size for w in weights))
         new = pl.pallas_call(
@@ -268,31 +303,32 @@
             in_specs=[hbm] * 12,
             out_specs=[vmem] * 9,
             scratch_shapes=[
-                *(pltpu.VMEM((LAYERS, 2, *b[1:]), BF16) for b in blocks),
-                *(pltpu.VMEM(b, BF16) for b in blocks),
-                *(pltpu.VMEM(b, BF16) for b in blocks),
+                pltpu.VMEM((4, 16, blocks[0][2]), F32),
+                pltpu.VMEM((4, 16, blocks[2][2]), F32),
                 pltpu.VMEM((16, 256), F32),
                 pltpu.VMEM((DEVICES, 8, 128), F32),
                 dma((6, 15)),
                 dma((6, 15)),
                 dma((6, 8)),
-                dma((3, 3)),
+                dma((3, 2)),
+                dma((2, 4)),
                 dma((DEVICES,)),
                 dma((DEVICES,)),
+                pltpu.SemaphoreType.REGULAR((6, 2)),
             ],
-            compiler_params=pltpu.CompilerParams(collective_id=0, has_side_effects=True, vmem_limit_bytes=12 * 2**20),
+            compiler_params=pltpu.CompilerParams(collective_id=0, has_side_effects=True, vmem_limit_bytes=5 * 2**18),
             name="step",
-        )(*arrays)
+        )(*(pltpu.with_memory_space_constraint(a, pltpu.HBM) for a in arrays))
         return tuple(
             pl.pallas_call(
                 write_kernel,
                 out_shape=[jax.ShapeDtypeStruct(one.shape, one.dtype) for one in new],
-                in_specs=[hbm] * 9,
+                in_specs=[vmem] * 9,
                 out_specs=[hbm] * 9,
                 scratch_shapes=[dma((9, LAYERS))],
-                compiler_params=pltpu.CompilerParams(vmem_limit_bytes=2**20),
+                compiler_params=pltpu.CompilerParams(vmem_limit_bytes=2**18),
                 name="write",
-            )(*new)
+            )(*(pltpu.with_memory_space_constraint(a, pltpu.VMEM) for a in new))
         )
 
     all_of, cut = P(None, None, None), P(None, "dp", None)

time: 324 us -> 294 us (0.907)
  local copies, waits for them, and re-layouts: 30 us -> 0 us
    unnamed x12 -> x0, local copies, waits for them, and re-layouts: 30 us -> none
where the time goes in v2:
time: 294 us
  Pallas kernels  293 us (100%)
    pallas_call x1, Pallas kernels, step(): pl.pallas_call(functools.partial(step_kernel, count), out_shape=new, in_s...  277 us
    pallas_call x1, Pallas kernels, step(): pl.pallas_call(write_kernel, out_shape=[jax.ShapeDtypeStruct(one.shape, o...  16.4 us

profile of v2, /device:TPU:0, one launch (start us, length us, event | category | flops | bytes accessed | tf_op | source)
XLA Modules:
  0.0 293.9 jit_solution(14140395597110018660)
XLA Ops:
  0.6 276.8 %step.1 = (bf16[2,1024,3328]{2,1,0:T(8,128)(2,1)S(1)}, bf16[2,1024,3328]{2,1,0:T(8,128)(2,1)S(1)}, bf16[2,3328,1024]{2,1,0:T(8,128)(2,1)S(1)}, f32[2,64,3328]{2,...) custom-call(bf16[1,2,1024,3328]{3,2,1,0:T(8,128)(2,1)} %refs_0_.1, ...), custom_call_target="tpu_custom_call" | custom-call | tf_op jit(solution)/shard_map/step/pallas_call | solution.py:300
  277.5 16.4 %write.1 = (bf16[2,1024,3328]{2,1,0:T(8,128)(2,1)}, bf16[2,1024,3328]{2,1,0:T(8,128)(2,1)}, bf16[2,3328,1024]{2,1,0:T(8,128)(2,1)}, f32[2,64,3328]{2,1,0:T(8,128...) custom-call(bf16[2,1024,3328]{2,1,0:T(8,128)(2,1)S(1)} %get-tuple-el, ...), custom_call_target="tpu_custom_call" | custom-call | tf_op jit(solution)/shard_map/write/pallas_call | solution.py:323

commit v3 on v2

--- a/solution.py
+++ b/solution.py
@@ -12,6 +12,8 @@
 WINDOW = 12
 BF16, F32 = jnp.bfloat16, jnp.float32
 AXES = ((0, 1, 2), (1, 2, 0), (2, 0, 1))
+WIDTH = 1664
+PIECES = 4
 UNITS = [(layer, w) for layer in range(LAYERS) for w in range(3)]
 
 
@@ -43,19 +45,24 @@
     return (w - 0.02 * step).astype(BF16), m, v
 
 
-def tiles(rows, columns, body, init=None):
-    def step(i, carry):
-        for c in range(0, columns, 256):
-            carry = body(pl.ds(pl.multiple_of(i * 16, 16), 16), pl.ds(c, 256), carry)
-        return carry
-
-    return lax.fori_loop(0, rows // 16, step, init)
+def tiles(rows, columns, body):
+    width = WIDTH if columns % WIDTH == 0 else columns
+
+    def step(i, _):
+        for c in range(0, columns, width):
+            body(pl.ds(pl.multiple_of(i * 16, 16), 16), pl.ds(c, width))
+
+    lax.fori_loop(0, rows // 16, step, None)
+
+
+def each(n, body):
+    lax.fori_loop(0, n, lambda p, _: body(p), None)
 
 
 def step_kernel(count, *refs):
     g, wt, m_in, v_in = (refs[i : i + 3] for i in (0, 3, 6, 9))
     out, m, v = (refs[i : i + 3] for i in (12, 15, 18))
-    wide, tall, squares, all_squares, send_sem, recv_sem, load_sem, in_sem, tile_sem, sum_send, sum_recv, free_sem = refs[21:]
+    wide, tall, squares, all_squares, send_sem, recv_sem, load_sem, in_sem, tile_sem, sum_send, sum_recv, free_sem, cut_send, cut_recv = refs[21:]
     rows = [ref.shape[2] // DEVICES for ref in g]
     columns = [ref.shape[3] for ref in g]
 
@@ -84,22 +91,44 @@
             device_id_type=pl.DeviceIdType.MESH,
         )
 
+    def piece(w, ref, p):
+        return ref.at[:, pl.ds(pl.multiple_of(p * 256, 256), 256)] if w == 2 else ref.at[pl.ds(pl.multiple_of(p * 16, 16), 16)]
+
+    def cut_copy(kind, n, p, source, target, to, w=None):
+        w = n if w is None else w
+        return pltpu.make_async_remote_copy(
+            src_ref=piece(w, source, p),
+            dst_ref=piece(w, target, p),
+            send_sem=cut_send.at[kind, n, p],
+            recv_sem=cut_recv.at[kind, n, p],
+            device_id={"dp": me + to},
+            device_id_type=pl.DeviceIdType.MESH,
+        )
+
     def load(w, layer, slot):
         source = g[w].at[0, layer, block(w, me + away(w, slot))]
         return pltpu.make_async_copy(source, part(w, layer, slot + 4), load_sem.at[layer * 3 + w, slot])
 
     def swap(w, layer, slot):
         source = g[w].at[0, layer, block(w, me + other + away(w, slot))]
-        return copy(w, layer, slot, source, part(w, layer, slot), other)
+        if (layer, slot) == (0, 7):
+            return PIECES, lambda p: cut_copy(0, w, p, source, part(w, layer, slot), other)
+        return 1, lambda p: copy(w, layer, slot, source, part(w, layer, slot), other)
 
     def first(w, layer, slot):
-        return copy(w, layer, 8 + slot - 4, part(w, layer, 4 + slot), part(w, layer, 8 + slot), hop[AXES[w][0]])
+        source, target, to = part(w, layer, 4 + slot), part(w, layer, 8 + slot), hop[AXES[w][0]]
+        if (layer, slot) == (0, 7):
+            return PIECES, lambda p: cut_copy(1, w, p, source, target, to)
+        return 1, lambda p: copy(w, layer, 8 + slot - 4, source, target, to)
 
     def second(w, layer, slot):
         return copy(w, layer, 12 + slot - 2, part(w, layer, slot), part(w, layer, 8 + slot), hop[AXES[w][1]])
 
     def third(w, layer):
-        return copy(w, layer, 14, part(w, layer, 1), part(w, layer, 9), hop[AXES[w][2]])
+        source, target, to = part(w, layer, 1), part(w, layer, 9), hop[AXES[w][2]]
+        if layer == LAYERS - 1:
+            return PIECES, lambda p: cut_copy(2, w, p, source, target, to)
+        return 1, lambda p: copy(w, layer, 14, source, target, to)
 
     early = [(w, layer, slot) for layer in range(LAYERS) for slot in (7, 6, 5, 4) for w in range(3)]
     late = [(w, layer, slot) for pair in ((3, 2), (1,), (0,)) for layer in range(LAYERS) for slot in pair for w in range(3)]
@@ -112,27 +141,54 @@
     pl.semaphore_wait(barrier, 4)
 
     swaps = [swap(*unit) for unit in early + late]
-    for c in swaps[:WINDOW]:
-        c.start()
-
-    def total(w, sources, target):
-        def tile(r, c, carry):
-            acc = sources[0][r, c].astype(F32)
-            for s in sources[1:]:
-                acc += s[r, c].astype(F32)
-            target[r, c] = acc.astype(BF16)
-            return carry
-
-        tiles(rows[w], columns[w], tile)
+    for p in range(PIECES):
+        for w in range(3):
+            swaps[w][1](p).start()
+    for _, c in swaps[3:WINDOW]:
+        c(0).start()
+
+    def done(copies, side):
+        n, c = copies
+        if n == 1:
+            getattr(c(0), side)()
+        else:
+            each(n, lambda p: getattr(c(p), side)())
+
+    def add_up(sources, r, c):
+        acc = sources[0][r, c].astype(F32)
+        for s in sources[1:]:
+            acc += s[r, c].astype(F32)
+        return acc
+
+    def total(sources, target):
+        def tile(r, c):
+            target[r, c] = add_up(sources, r, c).astype(BF16)
+
+        tiles(*target.shape, tile)
+
+    def join(w, layer, slot, p, swap_copy, first_copy):
+        swap_copy.wait_recv()
+        mine, theirs = part(w, layer, 4 + slot), part(w, layer, slot)
+        if p is not None:
+            mine, theirs = piece(w, mine, p), piece(w, theirs, p)
+        total([mine, theirs], mine)
+        first_copy.start()
+
+    for w in range(3):
+        load(w, 0, 7).wait()
+
+    @functools.partial(each, PIECES)
+    def _(p):
+        for w in range(3):
+            join(w, 0, 7, p, swaps[w][1](p), first(w, 0, 7)[1](p))
 
     for i, (w, layer, slot) in enumerate(early):
-        load(w, layer, slot).wait()
-        swaps[i].wait_recv()
-        total(w, [part(w, layer, 4 + slot), part(w, layer, slot)], part(w, layer, 4 + slot))
-        first(w, layer, slot).start()
+        if i >= 3:
+            load(w, layer, slot).wait()
+            join(w, layer, slot, None, swaps[i][1](0), first(w, layer, slot)[1](0))
         load(w, layer, slot - 4).start()
         if i + WINDOW < len(swaps):
-            swaps[i + WINDOW].start()
+            swaps[i + WINDOW][1](0).start()
 
     loads = [pltpu.make_async_copy(m_in[w], m[w], in_sem.at[w, 0]) for w in range(3)]
     for c in loads:
@@ -153,45 +209,71 @@
             freed.add(layer)
             for x in range(3):
                 for sent_slot in (7, 6, 5):
-                    first(x, layer, sent_slot).wait_send()
+                    done(first(x, layer, sent_slot), "wait_send")
                 for axis in (1, 2):
                     to = {"dp": me + hop[AXES[x][axis]]}
                     pl.semaphore_signal(free_sem.at[layer * 3 + x, axis - 1], inc=1, device_id=to, device_id_type=pl.DeviceIdType.MESH)
         load(w, layer, slot).wait()
-        swaps[i].wait_recv()
-        first(w, layer, slot + 4).wait_recv()
+        done(swaps[i], "wait_recv")
+        done(first(w, layer, slot + 4), "wait_recv")
         sources = [part(w, layer, slot + 4), part(w, layer, slot), part(w, layer, 12 + slot)]
         if slot < 2:
             second(w, layer, slot + 2).wait_recv()
             sources.append(part(w, layer, 10 + slot))
         if slot == 0:
-            third(w, layer).wait_recv()
-            sources.append(part(w, layer, 9))
-
-            def tile(r, c, carry, sources=sources, w=w, layer=layer):
-                acc = sources[0][r, c].astype(F32)
-                for s in sources[1:]:
-                    acc += s[r, c].astype(F32)
-                rounded = acc.astype(BF16).astype(F32)
-                v[w][layer, r, c] = rounded
-                return carry + rounded * rounded
-
-            squares[...] += tiles(rows[w], columns[w], tile, jnp.zeros((16, 256), F32))
+
+            def tile(r, c, sources=sources, w=w, layer=layer):
+                v[w][layer, r, c] = add_up(sources, r, c)
+
+            tiles(rows[w], columns[w], tile)
+        elif slot == 1:
+            pl.semaphore_wait(free_sem.at[layer * 3 + w, 1], 1)
+            n, c = third(w, layer)
+            target = part(w, layer, slot)
+            if n == 1:
+                total(sources, target)
+                c(0).start()
+            else:
+
+                @functools.partial(each, n)
+                def _(p, w=w, c=c, sources=sources, target=target):
+                    total([piece(w, ref, p) for ref in sources], piece(w, target, p))
+                    c(p).start()
+
         else:
-            total(w, sources, part(w, layer, slot))
-            if slot in (3, 1):
-                pl.semaphore_wait(free_sem.at[layer * 3 + w, int(slot == 1)], 1)
-            (third(w, layer) if slot == 1 else second(w, layer, slot)).start()
+            total(sources, part(w, layer, slot))
+            if slot == 3:
+                pl.semaphore_wait(free_sem.at[layer * 3 + w, 0], 1)
+            second(w, layer, slot).start()
         if i + WINDOW < len(swaps):
-            swaps[i + WINDOW].start()
-
-    for c in swaps:
-        c.wait_send()
+            swaps[i + WINDOW][1](0).start()
+
+    def finish(w, last, grad):
+        def tile(r, c):
+            rounded = (grad[r, c] + last[r, c].astype(F32)).astype(BF16).astype(F32)
+            grad[r, c] = rounded
+            squares[:, : c.size] += rounded * rounded
+
+        tiles(*last.shape, tile)
+
+    squares[...] = jnp.zeros_like(squares)
+    for w in range(3):
+        done(third(w, 0), "wait_recv")
+        finish(w, part(w, 0, 9), v[w].at[0])
+
+    @functools.partial(each, PIECES)
+    def _(p):
+        for w in range(3):
+            third(w, 1)[1](p).wait_recv()
+            finish(w, piece(w, part(w, 1, 9), p), piece(w, v[w].at[1], p))
+
+    for copies in swaps:
+        done(copies, "wait_send")
     for layer, w in UNITS:
-        first(w, layer, 4).wait_send()
-    for w, layer, slot in late:
-        if slot:
-            (third(w, layer) if slot == 1 else second(w, layer, slot)).wait_send()
+        done(first(w, layer, 4), "wait_send")
+        for slot in (3, 2):
+            second(w, layer, slot).wait_send()
+        done(third(w, layer), "wait_send")
 
     everyone = [
         pltpu.make_async_remote_copy(
@@ -204,9 +286,8 @@
         )
         for k in range(1, DEVICES)
     ]
-    s = squares[...]
-    s = s[:8] + s[8:]
-    all_squares[0] = s[:, :128] + s[:, 128:]
+    s = squares[:8] + squares[8:]
+    all_squares[0] = sum(s[:, c : c + 128] for c in range(0, WIDTH, 128))
     for c in everyone:
         c.start()
     loads += [pltpu.make_async_copy(wt[w].at[:, block(w, me)], out[w].at[:, block(w, me)], in_sem.at[w, 1]) for w in range(3)]
@@ -222,6 +303,18 @@
     def forward(w, layer, k, bit):
         where = out[w].at[layer, block(w, me + away(w, k))]
         return copy(w, layer, 7 + k if bit == 3 else (k | 1 << bit) - 1, where, where, other if bit == 3 else hop[AXES[w][2 - bit]])
+
+    def forward_cut(w, layer, k, bit, p):
+        where = out[w].at[layer, block(w, me + away(w, k))]
+        to = other if bit == 3 else hop[AXES[w][2 - bit]]
+        if k:
+            return cut_copy(3 + (bit == 3), w, p, where, where, to)
+        return cut_copy(5, bit, p, where, where, to, 0)
+
+    def arrived_cut(w, layer, k, p):
+        source, target = out[w].at[layer, block(w, me)], out[w].at[layer, block(w, me + away(w, k))]
+        kind, n = (5, k.bit_length() - 1) if layer == 0 else (3, w)
+        return cut_copy(kind, n, p, source, target, hop[AXES[w][3 - k.bit_length()]], w)
 
     def arrived(w, layer, k):
         bit = k.bit_length() - 1
@@ -265,17 +358,57 @@
                     tile_load(w, layer + 1, ahead - rows[w] // 16, slot).start()
 
     for layer, w in UNITS:
-        lax.fori_loop(0, rows[w] // 16, lambda i, _, w=w, layer=layer: advance(w, layer, i), None)
-        pass_on(w, layer, 0)
-    for layer, w, k in gather_order():
-        arrived(w, layer, k).wait_recv()
-        pass_on(w, layer, k)
+        if (layer, w) == (0, 0):
+
+            @functools.partial(each, PIECES)
+            def _(p):
+                advance(0, 0, p)
+                for bit in range(3):
+                    forward_cut(0, 0, 0, bit, p).start()
+
+            sent.append(forward(w, layer, 0, 3))
+            sent[-1].start()
+        else:
+            lax.fori_loop(0, rows[w] // 16, lambda i, _, w=w, layer=layer: advance(w, layer, i), None)
+            pass_on(w, layer, 0)
+    order = gather_order()
+    last = [(LAYERS - 1, w, 7) for w in range(3)]
+    assert sorted(order[-3:]) == last
+    for layer, w, k in order[:-3]:
+        if (layer, w) == (0, 0) and k & k - 1 == 0:
+            each(PIECES, lambda p, k=k: arrived_cut(0, 0, k, p).wait_recv())
+        else:
+            arrived(w, layer, k).wait_recv()
+        if (layer, k) == (LAYERS - 1, 3):
+            each(PIECES, lambda p, w=w: forward_cut(w, 1, 3, 2, p).start())
+            sent.append(forward(w, layer, k, 3))
+            sent[-1].start()
+        else:
+            pass_on(w, layer, k)
+
+    @functools.partial(each, PIECES)
+    def _(p):
+        for w in range(3):
+            arrived_cut(w, 1, 7, p).wait_recv()
+            forward_cut(w, 1, 7, 3, p).start()
+
     for layer, w in UNITS:
         for k in range(8):
             where = out[w].at[layer, block(w, me + other + away(w, k))]
-            copy(w, layer, 7 + k, where, where, other).wait_recv()
+            if (layer, w, k) in last:
+                each(PIECES, lambda p, w=w, where=where: cut_copy(4, w, p, where, where, other).wait_recv())
+            else:
+                copy(w, layer, 7 + k, where, where, other).wait_recv()
     for c in sent:
         c.wait_send()
+
+    @functools.partial(each, PIECES)
+    def _(p):
+        for n in range(3):
+            forward_cut(0, 0, 0, n, p).wait_send()
+            forward_cut(n, 1, 3, 2, p).wait_send()
+            forward_cut(n, 1, 7, 3, p).wait_send()
+
     for c in everyone:
         c.wait_send()
 
@@ -305,7 +438,7 @@
             scratch_shapes=[
                 pltpu.VMEM((4, 16, blocks[0][2]), F32),
                 pltpu.VMEM((4, 16, blocks[2][2]), F32),
-                pltpu.VMEM((16, 256), F32),
+                pltpu.VMEM((16, WIDTH), F32),
                 pltpu.VMEM((DEVICES, 8, 128), F32),
                 dma((6, 15)),
                 dma((6, 15)),
@@ -315,8 +448,10 @@
                 dma((DEVICES,)),
                 dma((DEVICES,)),
                 pltpu.SemaphoreType.REGULAR((6, 2)),
+                dma((6, 3, PIECES)),
+                dma((6, 3, PIECES)),
             ],
-            compiler_params=pltpu.CompilerParams(collective_id=0, has_side_effects=True, vmem_limit_bytes=5 * 2**18),
+            compiler_params=pltpu.CompilerParams(collective_id=0, has_side_effects=True, vmem_limit_bytes=2 * 2**20),
             name="step",
         )(*(pltpu.with_memory_space_constraint(a, pltpu.HBM) for a in arrays))
         return tuple(

time: 294 us -> 292 us (level)
  no operation moved by 1% of the time
where the time goes in v3:
time: 292 us; the launch traced here: 291 us
  Pallas kernels  291 us (100%)
    pallas_call x1, Pallas kernels, step(): pl.pallas_call(functools.partial(step_kernel, count), out_shape=new, in_s...  274 us
    pallas_call x1, Pallas kernels, step(): pl.pallas_call(write_kernel, out_shape=[jax.ShapeDtypeStruct(one.shape, o...  16.4 us

profile of v3, /device:TPU:0, one launch (start us, length us, event | category | flops | bytes accessed | tf_op | source)
XLA Modules:
  0.0 291.3 jit_solution(15802412465514882447)
XLA Ops:
  0.6 274.3 %step.1 = (bf16[2,1024,3328]{2,1,0:T(8,128)(2,1)S(1)}, bf16[2,1024,3328]{2,1,0:T(8,128)(2,1)S(1)}, bf16[2,3328,1024]{2,1,0:T(8,128)(2,1)S(1)}, f32[2,64,3328]{2,...) custom-call(bf16[1,2,1024,3328]{3,2,1,0:T(8,128)(2,1)} %refs_0_.1, ...), custom_call_target="tpu_custom_call" | custom-call | tf_op jit(solution)/shard_map/step/pallas_call | solution.py:433
  274.9 16.4 %write.1 = (bf16[2,1024,3328]{2,1,0:T(8,128)(2,1)}, bf16[2,1024,3328]{2,1,0:T(8,128)(2,1)}, bf16[2,3328,1024]{2,1,0:T(8,128)(2,1)}, f32[2,64,3328]{2,1,0:T(8,128...) custom-call(bf16[2,1024,3328]{2,1,0:T(8,128)(2,1)S(1)} %get-tuple-el, ...), custom_call_target="tpu_custom_call" | custom-call | tf_op jit(solution)/shard_map/write/pallas_call | solution.py:458
